TPU v7x, 128 devices: a whole 4x4x4 slice. The times are simulated.
128 devices in a mesh: dp: 32 (over x, z, core), tp: 4 (over y).
Axes of the slice: x: 4, y: 4, z: 4, core: 2. Of those that a mesh axis runs over, the one named last changes fastest.
Arguments:
- hidden_in: bfloat16 [2048, 3584], P(('dp', 'tp')), may hold values from -6 to 6
- query_latent: bfloat16 [2048, 64, 512], P(('dp', 'tp')), may hold values from -348 to 347
- query_rope: bfloat16 [2048, 4096], P(('dp', 'tp')), may hold values from -348 to 347
- cache_latent: bfloat16 [2048, 128, 512], P(('dp', 'tp')), may hold values from -6 to 6
- cache_rope: bfloat16 [2048, 64, 128], P(('dp', 'tp')), may hold values from -6 to 6
- lengths: int32 [2048], P(('dp', 'tp')), may hold values from 16 to 128
- value_up: bfloat16 [512, 4096], P(None, 'tp'), may hold values from -1 to 1
- out_proj: bfloat16 [4096, 3584], P('tp'), may hold values from -0.09375 to 0.09375
- norm_gain: float32 [3584], replicated, may hold values from 0.1 to 1.9
- expert_gate: bfloat16 [128, 3584, 1024], P(('dp', 'tp')), may hold values from -0.09375 to 0.09375
- expert_down: bfloat16 [128, 1024, 3584], P(('dp', 'tp')), may hold values from -0.1875 to 0.1875
- expert_ids: int32 [2048, 8], P(('dp', 'tp')), may hold values from 0 to 127, all different within a row; in each aligned block of 16 rows (0 to 15, 16 to 31, ...) at most 2 rows name the same one
- affinity: float32 [2048, 8], P(('dp', 'tp')), may hold values from 0.05 to 1
Outputs:
- layer_out: bfloat16 [2048, 3584], P(('dp', 'tp'))
Inputs may be any that keep to these rules, and one draw needn't show every extreme that they name: `expert_ids`: in each aligned block of 16 rows (the rows of one device) no expert is named by more than 2 rows.
All inputs are finite; a program needn't handle non-finite values.
Results may differ from a plain program's by a relative error of at most 0.0081.
Values may be sent and summed in bfloat16 or wider, within the bound.
A program may use at most 128 MiB of HBM per device.

v0:
```python
import jax
import jax.numpy as jnp
from jax import lax
from jax.sharding import PartitionSpec as P

score_scale = 192.0 ** (-0.5)
norm_eps = 1e-06
route_scale = 2.5


def in_blocks(shard, dim, peers):
    before, after = (shard.shape[:dim], shard.shape[dim + 1 :])
    return jnp.moveaxis(shard.reshape(*before, peers, -1, *after), dim, 0)


def sum_at_owner(shard, axis, dim):
    peers = lax.axis_size(axis)
    parts = lax.all_to_all(in_blocks(shard, dim, peers), axis, 0, 0, tiled=True)
    return jnp.sum(parts.astype(jnp.float32), axis=0)


def attend(query_latent, query_rope, cache_latent, cache_rope, lengths):
    token_count, head_count, latent_width = query_latent.shape
    rope_width = cache_rope.shape[1]
    context = cache_latent.shape[1]
    query_rot = query_rope.reshape(token_count, head_count, rope_width)
    scores = jnp.einsum(
        "thl,tpl->thp", query_latent, cache_latent, preferred_element_type=jnp.float32
    )
    scores = scores + jnp.einsum(
        "thr,trp->thp", query_rot, cache_rope, preferred_element_type=jnp.float32
    )
    scores = scores * score_scale
    position = lax.broadcasted_iota(jnp.int32, (token_count, 1, context), 2)
    scores = jnp.where(position < lengths[:, None, None], scores, -jnp.inf)
    row_max = jnp.max(scores, axis=2, keepdims=True)
    raised = jnp.exp(scores - row_max)
    attn_weights = (raised / jnp.sum(raised, axis=2, keepdims=True)).astype(jnp.bfloat16)
    latent_out = jnp.einsum(
        "thp,tpl->thl", attn_weights, cache_latent, preferred_element_type=jnp.float32
    )
    return latent_out.astype(jnp.bfloat16)


def per_device(
    hidden_in,
    query_latent,
    query_rope,
    cache_latent,
    cache_rope,
    lengths,
    value_up,
    out_proj,
    norm_gain,
    expert_gate,
    expert_down,
    expert_ids,
    affinity,
):
    latent_out = attend(query_latent, query_rope, cache_latent, cache_rope, lengths)
    group_size = lax.axis_size("tp")
    local_heads = latent_out.shape[1] // group_size
    by_heads = lax.all_to_all(latent_out, "tp", split_axis=1, concat_axis=0, tiled=True)
    head_width = value_up.shape[1] // local_heads
    up_table = value_up.reshape(value_up.shape[0], local_heads, head_width)
    per_head = jnp.einsum(
        "thl,lhv->thv", by_heads, up_table, preferred_element_type=jnp.float32
    ).astype(jnp.bfloat16)
    attn_sum = sum_at_owner(
        jnp.dot(
            per_head.reshape(hidden_in.shape[0] * lax.axis_size("tp"), local_heads * head_width),
            out_proj,
            preferred_element_type=jnp.float32,
        ).astype(jnp.bfloat16),
        "tp",
        0,
    )
    hidden = (hidden_in.astype(jnp.float32) + attn_sum).astype(jnp.bfloat16)
    wide_hidden = hidden.astype(jnp.float32)
    inv_norm = lax.rsqrt(jnp.mean(wide_hidden * wide_hidden, axis=1, keepdims=True) + norm_eps)
    normed = (wide_hidden * inv_norm * norm_gain).astype(jnp.bfloat16)
    tok_rows, top_count = expert_ids.shape
    width = normed.shape[1]
    experts = expert_gate.shape[0] * lax.axis_size("dp") * lax.axis_size("tp")
    capacity = max(2, -(-(tok_rows * top_count) // experts))
    flat_ids = expert_ids.reshape(-1)
    expert_iota = lax.broadcasted_iota(jnp.int32, (1, experts), 1)
    one_hot = (flat_ids[:, None] == expert_iota).astype(jnp.int32)
    earlier = jnp.cumsum(one_hot, axis=0) - one_hot
    slot_index = jnp.sum(earlier * one_hot, axis=1)
    target = flat_ids * capacity + slot_index
    owner_row = jnp.arange(tok_rows * top_count, dtype=jnp.int32) // top_count
    source_row = jnp.full((experts * capacity,), tok_rows, jnp.int32).at[target].set(owner_row)
    padded = jnp.concatenate([normed, jnp.zeros((1, width), jnp.bfloat16)], axis=0)
    outgoing = padded[source_row].reshape(experts, capacity, width)
    gate_local = expert_gate[0]
    down_local = expert_down[0]
    slot_rows = lax.all_to_all(outgoing, ("dp", "tp"), split_axis=0, concat_axis=0, tiled=True)
    lead_shape = slot_rows.shape[:-1]
    flat_rows = slot_rows.reshape(-1, width)
    inner_act = jax.nn.silu(
        jnp.dot(flat_rows, gate_local, preferred_element_type=jnp.float32)
    ).astype(jnp.bfloat16)
    answer = jnp.dot(inner_act, down_local, preferred_element_type=jnp.float32).astype(jnp.bfloat16)
    answered = answer.reshape(lead_shape + (width,))
    returned = lax.all_to_all(answered, ("dp", "tp"), split_axis=0, concat_axis=0, tiled=True)
    returned = returned.reshape(experts * capacity, width)
    picked = returned[target].reshape(tok_rows, top_count, width).astype(jnp.float32)
    route_weight = route_scale * affinity / jnp.sum(affinity, axis=1, keepdims=True)
    moe_sum = jnp.sum(picked * route_weight[:, :, None], axis=1)
    return (wide_hidden + moe_sum).astype(jnp.bfloat16)


def solution(mesh):
    return jax.shard_map(
        per_device,
        mesh=mesh,
        in_specs=(
            P(("dp", "tp"), None),
            P(("dp", "tp"), None, None),
            P(("dp", "tp"), None),
            P(("dp", "tp"), None, None),
            P(("dp", "tp"), None, None),
            P(("dp", "tp")),
            P(None, "tp"),
            P("tp", None),
            P(),
            P(("dp", "tp"), None, None),
            P(("dp", "tp"), None, None),
            P(("dp", "tp"), None),
            P(("dp", "tp"), None),
        ),
        out_specs=P(("dp", "tp"), None),
        check_vma=False,
    )
```

profile of v0, /device:TPU:1, one launch (start us, length us, event | category | flops | bytes accessed | tf_op | source)
XLA Modules:
  0.0 159.0 jit_solution(15531151931945262616)
XLA Ops:
  0.0 0.0 copy-start
  0.0 1.3 reshape.88
  1.3 0.7 iota_compare_fusion.1
  2.1 1.2 fusion.31
  3.2 2.1 %fusion.12 = f32[16,64,128]{2,1,0:T(8,128)S(1)} fusion(f32[16,64,128]{2,1,0:T(8,128)S(1)} %fusion.31, bf16[16,64,512]{2,1,0:T(8,128)(2,1)} %param.14, bf16[16,128,512]{2,1,0:T(8,128)(2,1)S(1)} %copy-done, pred[16,128]{1,0:T(8,128)(4,1)S(1)} %iota_compare_fusion.1), kind=kOutput, calls=%fused_computation.17 | convolution fusion | flops 134610944 | bytes 4196352 | tf_op jit(solution)/shard_map/thl,tpl->thp/dot_general | solution.py:27
  5.3 0.3 fusion.30
  5.7 3.0 %convolution_convert_fusion.1 = bf16[16,64,512]{2,1,0:T(8,128)(2,1)} fusion(bf16[16,128,512]{2,1,0:T(8,128)(2,1)S(1)} %copy-done, f32[16,64]{1,0:T(8,128)S(1)} %fusion.30, f32[16,64,128]{2,1,0:T(8,128)S(1)} %fusion.12), kind=kOutput, calls=%fused_computation.12 | convolution fusion | flops 135136384 | bytes 3674112 | tf_op jit(solution)/shard_map/thp,tpl->thl/dot_general | solution.py:39
  8.6 2.8 %copy.25 = bf16[16,64,512]{2,0,1:T(8,128)(2,1)} copy(bf16[16,64,512]{2,1,0:T(8,128)(2,1)} %convolution_convert_fusion.1) | data formatting | bytes 2097152 | tf_op jit(solution)/shard_map/convert_element_type | solution.py:42
  11.4 5.1 %all-to-all-start = ((bf16[16,64,512]{2,0,1:T(8,128)(2,1)}), bf16[16,64,512]{2,0,1:T(8,128)(2,1)S(1)}, u32[]{:S(2)}, u32[]{:S(2)}) async-start(bf16[16,64,512]{2,0,1:T(8,128)(2,1)} %copy.25), calls=%async_computation | async-start | bytes 2097152 | tf_op jit(solution)/shard_map/all_to_all | solution.py:63
  16.6 2.3 %copy.27 = bf16[512,1024]{0,1:T(8,128)(2,1)} copy(bf16[512,1024]{1,0:T(8,128)(2,1)} %param.19) | data formatting | bytes 2097152 | tf_op args[6]
  18.8 0.0 copy-done.3
  18.8 0.1 copy.30
  18.9 0.1 eq.15
  19.0 0.1 copy.29
  19.1 0.1 mul.71
  19.2 0.1 fusion.24
  19.3 0.2 reduce_window_sum.11
  19.4 0.2 select_reduce_fusion
  19.6 11.2 %all-to-all-done = bf16[16,64,512]{2,0,1:T(8,128)(2,1)S(1)} async-done(((bf16[16,64,512]{2,0,1:T(8,128)(2,1)}), bf16[16,64,512]{2,0,1:T(8,128)(2,1)S(1)}, u32[]{:S(2)}, u32[]{:S(2)}) %all-to-all-start) | async-done | bytes 1048608 | tf_op jit(solution)/shard_map/all_to_all | solution.py:63
  30.8 0.1 copy.26
  30.9 1.1 copy-done.1
  32.0 0.4 fusion.13
  32.4 0.2 copy.28
  32.6 0.2 reshape.90
  32.8 0.0 copy-start.2
  32.8 0.0 copy-start.5
  32.8 5.3 %convolution_convert_fusion = bf16[64,3584]{1,0:T(8,128)(2,1)} fusion(bf16[64,1024]{1,0:T(8,128)(2,1)S(1)} %reshape.90, bf16[1024,3584]{1,0:T(8,128)(2,1)} %param.20), kind=kOutput, calls=%fused_computation.9 | convolution fusion | flops 469991424 | bytes 7929856 | tf_op jit(solution)/shard_map/dot_general | solution.py:70
  38.1 3.5 %all-to-all-start.1 = ((bf16[4,16,3584]{2,1,0:T(8,128)(2,1)}), bf16[4,16,3584]{2,1,0:T(8,128)(2,1)S(1)}, u32[]{:S(2)}, u32[]{:S(2)}) async-start(bf16[4,16,3584]{2,1,0:T(8,128)(2,1)} %bitcast.5), calls=%async_computation.1 | async-start | bytes 917504 | tf_op jit(solution)/shard_map/all_to_all | solution.py:18
  41.6 1.0 scatter_custom_fusion
  42.6 5.7 %all-to-all-done.1 = bf16[4,16,3584]{2,1,0:T(8,128)(2,1)S(1)} async-done(((bf16[4,16,3584]{2,1,0:T(8,128)(2,1)}), bf16[4,16,3584]{2,1,0:T(8,128)(2,1)S(1)}, u32[]{:S(2)}, u32[]{:S(2)}) %all-to-all-start.1) | async-done | bytes 458784 | tf_op jit(solution)/shard_map/all_to_all | solution.py:18
  48.3 0.1 convert_reduce_fusion
  48.4 0.2 fusion.20
  48.6 0.0 copy-done.5
  48.6 0.1 fusion.22
  48.7 2.9 %gather_fusion = bf16[256,3584]{1,0:T(8,128)(2,1)} fusion(bf16[17,3584]{1,0:T(8,128)(2,1)S(1)} %concatenate.3, s32[1024]{0:T(1024)S(1)} %pad_clamp_fusion.1), kind=kCustom, calls=%fused_computation | custom fusion | bytes 3671040 | tf_op jit(solution)/shard_map/gather | solution.py:95
  51.6 4.8 %reshape.92 = bf16[128,2,3584]{2,1,0:T(2,128)(2,1)} reshape(bf16[256,3584]{1,0:T(8,128)(2,1)} %gather_fusion) | data formatting | bytes 3670016 | tf_op jit(solution)/shard_map/reshape | solution.py:95
  56.4 39.2 %all_to_all.33 = bf16[128,2,3584]{2,1,0:T(2,128)(2,1)} all-to-all(bf16[128,2,3584]{2,1,0:T(2,128)(2,1)} %reshape.92), channel_id=1, replica_groups=mesh['dp'=32,'tp'=4] {'dp','tp'}, dimensions={0} | all-to-all | bytes 3670016 | tf_op jit(solution)/shard_map/all_to_all | solution.py:98
  95.7 5.0 %reshape.93 = bf16[256,3584]{1,0:T(8,128)(2,1)} reshape(bf16[128,2,3584]{2,1,0:T(2,128)(2,1)} %all_to_all.33) | data formatting | bytes 3670016 | tf_op jit(solution)/shard_map/reshape | solution.py:100
  100.6 10.9 %fusion.5 = bf16[256,3584]{1,0:T(8,128)(2,1)} fusion(bf16[1,1024,3584]{2,1,0:T(8,128)(2,1)} %param.23, bf16[256,3584]{1,0:T(8,128)(2,1)} %reshape.93, bf16[1,3584,1024]{2,1,0:T(8,128)(2,1)} %param.22), kind=kOutput, calls=%fused_computation.8 | convolution fusion | flops 3760324608 | bytes 18350080 | tf_op jit(solution)/shard_map/dot_general | solution.py:104
  111.5 4.8 %reshape.94 = bf16[128,2,3584]{2,1,0:T(2,128)(2,1)} reshape(bf16[256,3584]{1,0:T(8,128)(2,1)} %fusion.5) | data formatting | bytes 3670016 | tf_op jit(solution)/shard_map/reshape | solution.py:105
  116.3 4.8 %all-to-all-start.3 = ((bf16[128,2,3584]{2,1,0:T(2,128)(2,1)}), bf16[128,2,3584]{2,1,0:T(2,128)(2,1)}, u32[]{:S(2)}, u32[]{:S(2)}) async-start(bf16[128,2,3584]{2,1,0:T(2,128)(2,1)} %reshape.94), calls=%async_computation.3 | async-start | bytes 3670016 | tf_op jit(solution)/shard_map/all_to_all | solution.py:106
  121.0 0.0 copy-done.4
  121.1 0.1 copy.31
  121.2 27.8 %all-to-all-done.3 = bf16[128,2,3584]{2,1,0:T(2,128)(2,1)} async-done(((bf16[128,2,3584]{2,1,0:T(2,128)(2,1)}), bf16[128,2,3584]{2,1,0:T(2,128)(2,1)}, u32[]{:S(2)}, u32[]{:S(2)}) %all-to-all-start.3) | async-done | bytes 1835040 | tf_op jit(solution)/shard_map/all_to_all | solution.py:106
  149.0 4.9 %reshape.95 = bf16[256,3584]{1,0:T(8,128)(2,1)} reshape(bf16[128,2,3584]{2,1,0:T(2,128)(2,1)} %all-to-all-done.3) | data formatting | bytes 3670016 | tf_op jit(solution)/shard_map/reshape | solution.py:107
  153.9 3.8 %gather_fusion.1 = bf16[128,3584]{1,0:T(8,128)(2,1)S(1)} fusion(bf16[256,3584]{1,0:T(8,128)(2,1)} %reshape.95, s32[1024]{0:T(1024)S(1)} %pad_clamp_fusion), kind=kCustom, calls=%fused_computation.1 | custom fusion | bytes 1835520 | tf_op jit(solution)/shard_map/gather | solution.py:108
  157.7 0.7 fusion.8
  158.3 0.7 fusion.23
  (15 shorter events, 0.1 us)
Async XLA Ops:
  0.0 3.2 %copy-start = (bf16[16,128,512]{2,1,0:T(8,128)(2,1)S(1)}, bf16[16,128,512]{2,1,0:T(8,128)(2,1)}, u32[]{:S(2)}) copy-start(bf16[16,128,512]{2,1,0:T(8,128)(2,1)} %param.16) | copy-start | bytes 6291460
  11.4 7.4 %copy-start.3 = (s32[16,8]{0,1:T(8,128)S(1)}, s32[16,8]{0,1:T(8,128)}, u32[]{:S(2)}) copy-start(s32[16,8]{0,1:T(8,128)} %param.24) | copy-start | bytes 1540
  11.4 19.4 %all-to-all-start = ((bf16[16,64,512]{2,0,1:T(8,128)(2,1)}), bf16[16,64,512]{2,0,1:T(8,128)(2,1)S(1)}, u32[]{:S(2)}, u32[]{:S(2)}) async-start(bf16[16,64,512]{2,0,1:T(8,128)(2,1)} %copy.25), calls=%async_computation | async-start | bytes 2097152 | tf_op jit(solution)/shard_map/all_to_all | solution.py:63
  30.8 1.2 copy-start.1
  32.8 15.6 %copy-start.2 = (bf16[16,3584]{1,0:T(8,128)(2,1)S(1)}, bf16[16,3584]{1,0:T(8,128)(2,1)}, u32[]{:S(2)}) copy-start(bf16[16,3584]{1,0:T(8,128)(2,1)} %param.13) | copy-start | bytes 344068
  32.8 15.7 %copy-start.5 = (f32[3584]{0:T(1024)S(1)}, f32[3584]{0:T(1024)}, u32[]{:S(2)}) copy-start(f32[3584]{0:T(1024)} %param.21) | copy-start | bytes 43012
  38.1 10.2 %all-to-all-start.1 = ((bf16[4,16,3584]{2,1,0:T(8,128)(2,1)}), bf16[4,16,3584]{2,1,0:T(8,128)(2,1)S(1)}, u32[]{:S(2)}, u32[]{:S(2)}) async-start(bf16[4,16,3584]{2,1,0:T(8,128)(2,1)} %bitcast.5), calls=%async_computation.1 | async-start | bytes 917504 | tf_op jit(solution)/shard_map/all_to_all | solution.py:18
  116.3 4.8 %copy-start.4 = (f32[16,8]{0,1:T(8,128)S(1)}, f32[16,8]{0,1:T(8,128)}, u32[]{:S(2)}) copy-start(f32[16,8]{0,1:T(8,128)} %param.25) | copy-start | bytes 1540
  116.3 32.7 %all-to-all-start.3 = ((bf16[128,2,3584]{2,1,0:T(2,128)(2,1)}), bf16[128,2,3584]{2,1,0:T(2,128)(2,1)}, u32[]{:S(2)}, u32[]{:S(2)}) async-start(bf16[128,2,3584]{2,1,0:T(2,128)(2,1)} %reshape.94), calls=%async_computation.3 | async-start | bytes 3670016 | tf_op jit(solution)/shard_map/all_to_all | solution.py:106
where the time goes:
time: 160 us; the launch traced here: 159 us
  waiting for transfers between devices  44.7 us (28%)
  blocking collectives  39.2 us (25%)
  local copies, waits for them, and re-layouts  35.5 us (22%)
  matrix products  22.8 us (14%)
  starting transfers between devices  13.4 us (8%)
  other arithmetic  3.25 us (2%)
    all_to_all x1, blocking collectives, per_device(): lax.all_to_all(outgoing, ('dp', 'tp'), split_axis=0, concat_axis=0, tiled...  39.2 us
    all_to_all x1, waiting for transfers between devices, per_device(): lax.all_to_all(answered, ('dp', 'tp'), split_axis=0, concat_axis=0, tiled...  27.8 us
    all_to_all x1, waiting for transfers between devices, per_device(): lax.all_to_all(latent_out, 'tp', split_axis=1, concat_axis=0, tiled=True)  11.2 us
    dot_general x1, matrix products, per_device(): jnp.dot(inner_act, down_local, preferred_element_type=jnp.float32)  10.9 us
    all_to_all x1, waiting for transfers between devices, sum_at_owner(): parts = lax.all_to_all(in_blocks(shard, dim, peers), axis, 0, 0, tiled=True)  5.71 us
    dot_general x1, matrix products, per_device(): jnp.dot(per_head.reshape(hidden_in.shape[0] * lax.axis_size('tp'), local_...  5.27 us
    all_to_all x1, starting transfers between devices, per_device(): lax.all_to_all(latent_out, 'tp', split_axis=1, concat_axis=0, tiled=True)  5.14 us
    reshape x1, local copies, waits for them, and re-layouts, per_device(): flat_rows = slot_rows.reshape(-1, width)  4.95 us
  transfers between devices with their start and end apart: 3, of which 3 were waited for; matrix products, arithmetic and copies ran while one was open for 3% of the time, Pallas kernels for 0%

commit v1 on v0

v1 whole, which is shorter than its diff:
```python
import jax
import jax.numpy as jnp
from jax import lax
from jax.experimental import pallas as pl
from jax.experimental.pallas import tpu as pltpu
from jax.sharding import PartitionSpec as P

BF16 = jnp.bfloat16
F32 = jnp.float32
MESH = pl.DeviceIdType.MESH

score_scale = 192.0 ** (-0.5)
norm_eps = 1e-06
route_scale = 2.5

TOK, HEADS, LAT, ROPE, CTX = 16, 64, 512, 64, 128
D, FF, TOPK = 3584, 1024, 8
HLOC = 16
UPW = 1024
GROUP = 4
OUT_CHUNK = 512

DIMS = ((0, 1, 2), (1, 2, 0), (2, 0, 1))
CHUNKS = ((0, 1152, 0), (1152, 1280, 1), (2432, 1152, 2))
STRIDE = (32, 1, 8)


def dot(a, b):
    return jnp.dot(a, b, preferred_element_type=F32)


def dot_nt(a, b):
    return lax.dot_general(a, b, (((1,), (1,)), ((), ())), preferred_element_type=F32)


def iota(shape, dim):
    return lax.broadcasted_iota(jnp.int32, shape, dim)


def coords(row_order, j):
    d1, d2, d3 = DIMS[j]
    part = {d3: row_order // 64, d2: (row_order // 8) % 4, d1: (row_order // 2) % 4}
    return part[0], part[1], part[2], (row_order // 32) % 2, row_order % 2


def slot_index(x, y, z, c, s, j):
    pos = (x, y, z)
    d1, d2, d3 = DIMS[j]
    return pos[d3] * 64 + c * 32 + pos[d2] * 8 + pos[d1] * 2 + s


def layer_kernel(*refs):
    n_chunk = len(CHUNKS)
    it = iter(refs)

    def take(n):
        return [next(it) for _ in range(n)]

    (lens, hid_h, ql_h, qr_h, cl_h, cr_h, vu_h, op_h, ng_h, eg_h, ed_h, ids_h, aff_h) = take(13)
    (out,) = take(1)
    (hid, ql, qr, cl, cr, vu, op, ng, eg, ed, ids, aff) = take(12)
    (ls, lr, ph, ps, pr, hb, hacc) = take(7)
    (mt1, mt2, sel, whi, wlo) = take(5)
    gat = take(n_chunk)
    sx = take(n_chunk)
    ox = take(n_chunk)
    yx = take(n_chunk)
    qx = take(n_chunk)
    px = take(n_chunk)
    ux = take(n_chunk)
    tx = take(n_chunk)
    vx = take(n_chunk)
    (ld, lat_s, lat_r, rs_s, rs_r, m1_s, m1_r, m2_s, m2_r, ex_s, ex_r) = take(11)

    dp = lax.axis_index("dp")
    y = lax.axis_index("tp")
    x, z, c = dp // 8, (dp // 2) % 4, dp % 2
    pos = (x, y, z)
    me = (dp, y)

    def at(d, k, dc=0):
        q = [x, y, z]
        q[d] = (q[d] + k) % 4
        return ((q[0] * 4 + q[2]) * 2 + (c + dc) % 2, q[1])

    peers = [at(d, k, dc) for d in range(3) for k in (1, 2, 3) for dc in (0, 1)] + [at(0, 0, 1)]

    def remote(src, dst, s, r, to):
        return pltpu.make_async_remote_copy(
            src_ref=src, dst_ref=dst, send_sem=s, recv_sem=r, device_id=to, device_id_type=MESH
        )

    barrier = pltpu.get_barrier_semaphore()
    for peer in peers:
        pl.semaphore_signal(barrier, inc=1, device_id=peer, device_id_type=MESH)

    def load(src, dst, sem):
        copy = pltpu.make_async_copy(src, dst, ld.at[sem])
        copy.start()
        return copy

    groups = TOK // GROUP
    att_loads = []
    small = [load(ids_h, ids, 0), load(aff_h, aff, 1)]
    for g in range(groups):
        sl = pl.ds(g * GROUP, GROUP)
        att_loads.append(
            [
                load(ql_h.at[sl], ql.at[sl], 2 + 4 * g),
                load(cl_h.at[sl], cl.at[sl], 3 + 4 * g),
                load(qr_h.at[sl], qr.at[sl], 4 + 4 * g),
                load(cr_h.at[sl], cr.at[sl], 5 + 4 * g),
            ]
        )
    base = 2 + 4 * groups
    vu_load = load(vu_h, vu, base)
    op_load = load(op_h, op, base + 1)
    hid_load = load(hid_h, hid, base + 2)
    ng_load = load(ng_h, ng, base + 3)
    eg_load = load(eg_h.at[0], eg, base + 4)
    ed_load = load(ed_h.at[0], ed, base + 5)

    for copy in small:
        copy.wait()
    ids_f = ids[...].astype(F32)
    affinity = aff[...]
    weight = route_scale * affinity / jnp.sum(affinity, axis=1, keepdims=True)
    w_hi = weight.astype(BF16)
    w_lo = (weight - w_hi.astype(F32)).astype(BF16)
    spread = (iota((TOPK, 128), 1) % TOPK == iota((TOPK, 128), 0)).astype(F32).astype(BF16)
    own_lane = iota((TOK, 128), 1) // TOPK == iota((TOK, 128), 0)

    def to_lanes(v):
        return jnp.sum(jnp.where(own_lane, dot(v, spread), 0.0), axis=0, keepdims=True)

    ids_b = ids_f.astype(BF16)
    id_row = to_lanes(ids_b)
    rep = (iota((128, TOK), 0) // TOPK == iota((128, TOK), 1)).astype(F32).astype(BF16)
    id_col = jnp.sum(
        jnp.where(iota((128, TOPK), 0) % TOPK == iota((128, TOPK), 1), dot(rep, ids_b), 0.0),
        axis=1,
        keepdims=True,
    )
    earlier = (id_col == id_row) & (iota((128, 128), 0) < iota((128, 128), 1))
    slot_row = jnp.sum(jnp.where(earlier, 1.0, 0.0), axis=0, keepdims=True)
    mrow = iota((16, 128), 0)
    meta = jnp.where(
        mrow == 0,
        id_row,
        jnp.where(mrow == 1, slot_row, jnp.where(mrow == 2, to_lanes(w_hi), to_lanes(w_lo))),
    ).astype(BF16)
    for d in range(3):
        mt1[d, pos[d]] = meta

    position = iota((HEADS, CTX), 1)

    def attend(t):
        q, kv = ql[t], cl[t]
        scores = dot_nt(q, kv) + dot(qr[t], cr[t])
        scores = jnp.where(position < lens[t], scores * score_scale, -jnp.inf)
        raised = jnp.exp(scores - jnp.max(scores, axis=1, keepdims=True))
        probs = (raised / jnp.sum(raised, axis=1, keepdims=True)).astype(BF16)
        latent = dot(probs, kv).astype(BF16)
        for g in range(4):
            ls[g, t] = latent[g * HLOC : (g + 1) * HLOC]

    lat_sends = []
    for g in range(groups):
        for copy in att_loads[g]:
            copy.wait()

        def step(i, carry):
            for u in range(2):
                attend(g * GROUP + i * 2 + u)
            return carry

        lax.fori_loop(0, GROUP // 2, step, 0)
        if g == 0:
            pl.semaphore_wait(barrier, len(peers))
        for k in (2, 1, 3):
            to = at(1, k)
            copy = remote(
                ls.at[to[1], pl.ds(g * GROUP, GROUP)],
                lr.at[y, pl.ds(g * GROUP, GROUP)],
                lat_s.at[g, k],
                lat_r.at[g, k],
                to,
            )
            copy.start()
            lat_sends.append(copy)
        if g == 0:
            for d in range(3):
                for k in (1, 2, 3):
                    remote(mt1.at[d, pos[d]], mt1.at[d, pos[d]], m1_s.at[d], m1_r.at[d], at(d, k)).start()

    for j in range(3):
        d1, d2, _ = DIMS[j]
        remote(mt1.at[d1, pl.ds(0, 3)], mt1.at[d1, pl.ds(0, 3)], m1_s.at[d1], m1_r.at[d1], me).wait_recv()
        mt2[j, pos[d2]] = mt1[d1]
    for j in range(3):
        d1, d2, _ = DIMS[j]
        for k in (1, 2, 3):
            remote(mt2.at[j, pos[d2]], mt2.at[j, pos[d2]], m2_s.at[j], m2_r.at[j], at(d2, k)).start()

    vu_load.wait()
    diag = iota((TOK * HLOC, UPW), 0) % HLOC == iota((TOK * HLOC, UPW), 1) // 64
    fold = (iota((TOK, TOK * HLOC), 1) // HLOC == iota((TOK, TOK * HLOC), 0)).astype(F32).astype(BF16)

    def up(latents, src):
        wide = dot(latents.reshape(TOK * HLOC, LAT), vu[...])
        ph[src] = dot(fold, jnp.where(diag, wide, 0.0).astype(BF16)).astype(BF16)

    up(ls[y], y)

    row = iota((256, 128), 0)
    pick_row = iota((256, 256), 0)
    pick_col = iota((256, 256), 1)
    tok_of_lane = (iota((128, 256), 0) // TOPK == iota((128, 256), 1) % TOK).astype(F32).astype(BF16)
    tok_of_lane_t = (iota((256, 128), 1) // TOPK == iota((256, 128), 0) % TOK).astype(F32).astype(BF16)
    for j in range(3):
        _, _, d3 = DIMS[j]
        remote(mt2.at[j, pl.ds(0, 3)], mt2.at[j, pl.ds(0, 3)], m2_s.at[j], m2_r.at[j], me).wait_recv()
        facts = mt2[j].reshape(256, 128)

        def of_source(n):
            hot = pick_col == ((pick_row // 2) % 16) * 16 + n
            return dot(hot.astype(F32).astype(BF16), facts)

        here = sum(pos[d] * STRIDE[d] for d in range(3) if d != d3)
        expert = here + (row // 64) * STRIDE[d3] + ((row // 32) % 2) * 4
        match = (of_source(0) == expert.astype(F32)) & (of_source(1) == (row % 2).astype(F32))
        same = (pick_row // 2) % 16 == pick_col // TOK
        hit = jnp.where(match, 1.0, 0.0).astype(BF16)
        sel[j] = jnp.where(same, dot(hit, tok_of_lane), 0.0).astype(BF16)
        same_t = (pick_col // 2) % 16 == pick_row // TOK
        for n, ref in ((2, whi), (3, wlo)):
            val = jnp.where(match, of_source(n), 0.0).astype(BF16)
            ref[j] = jnp.where(same_t, dot_nt(tok_of_lane_t, val), 0.0).astype(BF16)

    for k in (1, 3, 2):
        for g in range(groups):
            sl = pl.ds(g * GROUP, GROUP)
            remote(ls.at[0, sl], lr.at[0, sl], lat_s.at[g, k], lat_r.at[g, k], me).wait_recv()
        src = (y + 4 - k) % 4
        up(lr[src], src)

    op_load.wait()
    heads_out = ph[...].reshape(4 * TOK, UPW)

    def project(n, carry):
        cols = pl.ds(pl.multiple_of(n * OUT_CHUNK, OUT_CHUNK), OUT_CHUNK)
        part = dot(heads_out, op[:, cols]).astype(BF16)
        ps[:, :, cols] = part.reshape(4, TOK, OUT_CHUNK)
        for k in (2, 1, 3):
            to = at(1, k)
            remote(ps.at[to[1], :, cols], pr.at[y, :, cols], rs_s, rs_r, to).start()
        return carry

    lax.fori_loop(0, D // OUT_CHUNK, project, 0)
    hid_load.wait()
    ng_load.wait()
    pr[y] = ps[y]
    remote(ps.at[pl.ds(0, 3)], pr.at[pl.ds(0, 3)], rs_s, rs_r, me).wait_recv()
    total = hid[...].astype(F32)
    for src in range(4):
        total = total + pr[src].astype(F32)
    hidden = total.astype(BF16)
    hid[...] = hidden
    wide = hidden.astype(F32)
    inv = lax.rsqrt(jnp.mean(wide * wide, axis=1, keepdims=True) + norm_eps)
    normed = (wide * inv * ng[...]).astype(BF16)

    def exchange(ph_no, i, src, dst, to):
        remote(src, dst, ex_s.at[ph_no, i], ex_r.at[ph_no, i], to).start()

    def arrived(ph_no, i, ref, n):
        remote(ref.at[pl.ds(0, n)], ref.at[pl.ds(0, n)], ex_s.at[ph_no, i], ex_r.at[ph_no, i], me).wait_recv()

    line = [(k, dc) for k in (2, 1, 3, 0) for dc in (0, 1) if (k, dc) != (0, 0)]

    def to_line(ph_no, i, d3, src, dst):
        slot = pos[d3] * 2 + c
        for k, dc in line:
            there = ((pos[d3] + k) % 4) * 2 + (c + dc) % 2
            exchange(ph_no, i, src.at[there], dst.at[slot], at(d3, k, dc))
        dst[slot] = src[slot]

    for i, (lo, n, j) in enumerate(CHUNKS):
        d1, d2, d3 = DIMS[j]
        gat[i][pos[d2], pos[d1]] = normed[:, lo : lo + n]
        for k in (2, 1, 3):
            mine = gat[i].at[pos[d2], pos[d1]]
            exchange(0, i, mine, mine, at(d1, k))
    for i, (lo, n, j) in enumerate(CHUNKS):
        d1, d2, d3 = DIMS[j]
        arrived(0, i, gat[i].at[0], 3)
        for k in (2, 1, 3):
            mine = gat[i].at[pos[d2]]
            exchange(1, i, mine, mine, at(d2, k))
    for i, (lo, n, j) in enumerate(CHUNKS):
        d1, d2, d3 = DIMS[j]
        arrived(1, i, gat[i], 3)
        rows = dot(sel[j], gat[i][...].reshape(256, n)).astype(BF16)
        sx[i][...] = rows.reshape(8, 32, n)
        to_line(2, i, d3, sx[i], ox[i])

    def reorder(to_j, from_j):
        want = slot_index(*coords(pick_row, to_j), from_j)
        return (want == pick_col).astype(F32).astype(BF16)

    eg_load.wait()
    for i, (lo, n, j) in enumerate(CHUNKS):
        arrived(2, i, ox[i], 7)
        rows = ox[i][...].reshape(256, n)
        if j != 0:
            rows = dot(reorder(0, j), rows).astype(BF16)
        part = dot(rows, eg[lo : lo + n, :])
        if i == 0:
            hacc[...] = part
        elif i < n_chunk - 1:
            hacc[...] += part
        else:
            v = hacc[...] + part
            hb[...] = (v / (1.0 + jnp.exp(-v))).astype(BF16)
    ed_load.wait()
    for i, (lo, n, j) in enumerate(CHUNKS):
        d1, d2, d3 = DIMS[j]
        rows = dot(hb[...], ed[:, lo : lo + n]).astype(BF16)
        if j != 0:
            rows = dot(reorder(j, 0), rows).astype(BF16)
        yx[i][...] = rows.reshape(8, 32, n)
        to_line(3, i, d3, yx[i], qx[i])

    for i, (lo, n, j) in enumerate(CHUNKS):
        d1, d2, d3 = DIMS[j]
        arrived(3, i, qx[i], 7)
        rows = qx[i][...].reshape(256, n)
        summed = (dot(whi[j], rows) + dot(wlo[j], rows)).astype(BF16)
        px[i][...] = summed.reshape(4, 64, n)
        for k in (2, 1, 3):
            exchange(4, i, px[i].at[(pos[d2] + k) % 4], ux[i].at[pos[d2]], at(d2, k))
        ux[i][pos[d2]] = px[i][pos[d2]]
    for i, (lo, n, j) in enumerate(CHUNKS):
        d1, d2, d3 = DIMS[j]
        arrived(4, i, ux[i], 3)
        acc = ux[i][0].astype(F32)
        for q in range(1, 4):
            acc = acc + ux[i][q].astype(F32)
        tx[i][...] = acc.astype(BF16).reshape(4, TOK, n)
        for k in (2, 1, 3):
            exchange(5, i, tx[i].at[(pos[d1] + k) % 4], vx[i].at[pos[d1]], at(d1, k))
        vx[i][pos[d1]] = tx[i][pos[d1]]
    for i, (lo, n, j) in enumerate(CHUNKS):
        arrived(5, i, vx[i], 3)
        acc = hid[:, lo : lo + n].astype(F32)
        for q in range(4):
            acc = acc + vx[i][q].astype(F32)
        out[:, lo : lo + n] = acc.astype(BF16)

    for copy in lat_sends:
        copy.wait_send()
    remote(ps.at[pl.ds(0, 3)], pr.at[pl.ds(0, 3)], rs_s, rs_r, me).wait_send()
    for d in range(3):
        remote(mt1.at[d, pl.ds(0, 3)], mt1.at[d, pl.ds(0, 3)], m1_s.at[d], m1_r.at[d], me).wait_send()
        remote(mt2.at[d, pl.ds(0, 3)], mt2.at[d, pl.ds(0, 3)], m2_s.at[d], m2_r.at[d], me).wait_send()
    for i in range(n_chunk):
        for ph_no, ref, n in (
            (0, gat[i].at[0], 3),
            (1, gat[i], 3),
            (2, sx[i], 7),
            (3, yx[i], 7),
            (4, px[i], 3),
            (5, tx[i], 3),
        ):
            part = ref.at[pl.ds(0, n)]
            remote(part, part, ex_s.at[ph_no, i], ex_r.at[ph_no, i], me).wait_send()


def per_device(
    hidden_in,
    query_latent,
    query_rope,
    cache_latent,
    cache_rope,
    lengths,
    value_up,
    out_proj,
    norm_gain,
    expert_gate,
    expert_down,
    expert_ids,
    affinity,
):
    n_chunk = len(CHUNKS)
    dma = pltpu.SemaphoreType.DMA
    v = pltpu.VMEM
    scratch = [
        v((TOK, D), BF16),
        v((TOK, HEADS, LAT), BF16),
        v((TOK, HEADS, ROPE), BF16),
        v((TOK, CTX, LAT), BF16),
        v((TOK, ROPE, CTX), BF16),
        v((LAT, UPW), BF16),
        v((UPW, D), BF16),
        v((1, D), F32),
        v((D, FF), BF16),
        v((FF, D), BF16),
        v((TOK, TOPK), jnp.int32),
        v((TOK, TOPK), F32),
        v((4, TOK, HLOC, LAT), BF16),
        v((4, TOK, HLOC, LAT), BF16),
        v((4, TOK, UPW), BF16),
        v((4, TOK, D), BF16),
        v((4, TOK, D), BF16),
        v((256, FF), BF16),
        v((256, FF), F32),
        v((3, 4, 16, 128), BF16),
        v((3, 4, 4, 16, 128), BF16),
        v((3, 256, 256), BF16),
        v((3, 256, 256), BF16),
        v((3, 256, 256), BF16),
    ]
    for shape in ((4, 4, TOK), (8, 32), (8, 32), (8, 32), (8, 32), (4, 64), (4, 64), (4, TOK), (4, TOK)):
        scratch += [v(shape + (n,), BF16) for _, n, _ in CHUNKS]
    scratch += [
        dma((2 + TOK + 6,)),
        dma((TOK // GROUP, 4)),
        dma((TOK // GROUP, 4)),
        dma,
        dma,
        dma((3,)),
        dma((3,)),
        dma((3,)),
        dma((3,)),
        dma((6, n_chunk)),
        dma((6, n_chunk)),
    ]
    anyspace = pl.BlockSpec(memory_space=pl.ANY)
    return pl.pallas_call(
        layer_kernel,
        out_shape=jax.ShapeDtypeStruct((TOK, D), BF16),
        in_specs=[pl.BlockSpec(memory_space=pltpu.SMEM)] + [anyspace] * 12,
        out_specs=pl.BlockSpec(memory_space=pltpu.VMEM),
        scratch_shapes=scratch,
        compiler_params=pltpu.CompilerParams(
            collective_id=0, has_side_effects=True, vmem_limit_bytes=64 * 1024 * 1024 - 65536
        ),
        name="layer",
    )(
        lengths,
        hidden_in,
        query_latent,
        query_rope.reshape(TOK, HEADS, ROPE),
        cache_latent,
        cache_rope,
        value_up,
        out_proj,
        norm_gain.reshape(1, D),
        expert_gate,
        expert_down,
        expert_ids,
        affinity,
    )


def solution(mesh):
    return jax.shard_map(
        per_device,
        mesh=mesh,
        in_specs=(
            P(("dp", "tp"), None),
            P(("dp", "tp"), None, None),
            P(("dp", "tp"), None),
            P(("dp", "tp"), None, None),
            P(("dp", "tp"), None, None),
            P(("dp", "tp")),
            P(None, "tp"),
            P("tp", None),
            P(),
            P(("dp", "tp"), None, None),
            P(("dp", "tp"), None, None),
            P(("dp", "tp"), None),
            P(("dp", "tp"), None),
        ),
        out_specs=P(("dp", "tp"), None),
        check_vma=False,
    )
```

time: 160 us -> 91 us (0.57)
  Pallas kernels: 0 us -> 83.1 us
  waiting for transfers between devices: 44.7 us -> 0 us
  blocking collectives: 39.2 us -> 0 us
  local copies, waits for them, and re-layouts: 35.5 us -> 7.46 us
  matrix products: 22.8 us -> 0 us
  starting transfers between devices: 13.4 us -> 0 us
  other arithmetic: 3.25 us -> 0 us
    pallas_call x0 -> x1, Pallas kernels: none -> 83.1 us  [per_device(): pl.pallas_call(layer_kernel, out_shape=jax.ShapeDtypeStruct((TOK, D), BF1...]
    all_to_all x3 -> x0, waiting for transfers between devices: 44.7 us -> none  [the longest x1 27.8 us: per_device(): lax.all_to_all(answered, ('dp', 'tp'), split_axis=0, concat_axis=0, tiled...]
    all_to_all x1 -> x0, blocking collectives: 39.2 us -> none  [per_device(): lax.all_to_all(outgoing, ('dp', 'tp'), split_axis=0, concat_axis=0, tiled...]
    dot_general x6 -> x0, matrix products: 22.8 us -> none  [the longest x1 10.9 us: per_device(): jnp.dot(inner_act, down_local, preferred_element_type=jnp.float32)]
    reshape x6 -> x2, local copies, waits for them, and re-layouts: 20.9 us -> 3.21 us  [the longest x1 1.88 us: per_device(): query_rope.reshape(TOK, HEADS, ROPE)]
    all_to_all x3 -> x0, starting transfers between devices: 13.4 us -> none  [the longest x1 5.14 us: per_device(): lax.all_to_all(latent_out, 'tp', split_axis=1, concat_axis=0, tiled=True)]
    gather x2 -> x0, local copies, waits for them, and re-layouts: 6.71 us -> none  [the longest x1 3.76 us: per_device(): returned[target].reshape(tok_rows, top_count, width).astype(jnp.float32)]
    convert_element_type x2 -> x0, local copies, waits for them, and re-layouts: 2.97 us -> none  [the longest x1 2.79 us: attend(): return latent_out.astype(jnp.bfloat16)]
  transfers between devices with their start and end apart: 3 -> 0, of which waited for: 3 -> 0; matrix products, arithmetic and copies ran while one was open for 3% -> 0% of each run, Pallas kernels for 0% -> 0%
where the time goes in v1:
time: 91 us; the launch traced here: 90.5 us
  Pallas kernels  83.1 us (91%)
  local copies, waits for them, and re-layouts  7.46 us (8%)
    pallas_call x1, Pallas kernels, per_device(): pl.pallas_call(layer_kernel, out_shape=jax.ShapeDtypeStruct((TOK, D), BF1...  83.1 us
    unnamed x3, local copies, waits for them, and re-layouts  4.26 us
    reshape x1, local copies, waits for them, and re-layouts, per_device(): query_rope.reshape(TOK, HEADS, ROPE)  1.88 us

profile of v1, /device:TPU:1, one launch (start us, length us, event | category | flops | bytes accessed | tf_op | source)
XLA Modules:
  0.0 90.5 jit_solution(3466428708688697590)
XLA Ops:
  0.0 1.4 %copy.14.refs_11_ = s32[16,8]{1,0:T(8,128)} copy(s32[16,8]{0,1:T(8,128)} %param.24) | data formatting | bytes 1024 | tf_op args[11]
  1.4 1.4 %copy.15.refs_12_ = f32[16,8]{1,0:T(8,128)} copy(f32[16,8]{0,1:T(8,128)} %param.25) | data formatting | bytes 1024 | tf_op args[12]
  2.7 1.3 %reshape.7.refs_8_ = f32[1,3584]{1,0:T(1,128)} reshape(f32[3584]{0:T(1024)} %param.21) | data formatting | bytes 28672 | tf_op jit(solution)/shard_map/reshape | solution.py:458
  4.0 1.9 %reshape.6.refs_3_ = bf16[16,64,64]{2,1,0:T(8,128)(2,1)} reshape(bf16[16,4096]{1,0:T(8,128)(2,1)} %param.15) | data formatting | bytes 262144 | tf_op jit(solution)/shard_map/reshape | solution.py:453
  5.9 83.1 %layer.1 = bf16[16,3584]{1,0:T(8,128)(2,1)} custom-call(s32[16]{0:T(128)} %refs_0_.1, bf16[16,3584]{1,0:T(8,128)(2,1)} %refs_1_.1, bf16[16,64,512]{2,1,0:T(8,128)(2,1)} %refs_2_.1, bf16[16,64,64]{2,1,0:T(8,128)(2,1)} %reshape.6.refs_3_, bf16[16,128,512]{2,1,0:T(8,128)(2,1)} %refs_4_.1, bf16[16,64,128]{2,1,0:T(8,128)(2,1)} %refs_5_.1, ...), custom_call_target="tpu_custom_call" | custom-call | tf_op jit(solution)/shard_map/layer/pallas_call | solution.py:439
  89.0 1.6 %copy.17 = bf16[16,3584]{1,0:T(8,128)(2,1)} copy(bf16[16,3584]{1,0:T(8,128)(2,1)} %layer.1) | data formatting | bytes 229376

commit v2 on v1

--- a/solution.py
+++ b/solution.py
@@ -17,11 +17,15 @@
 D, FF, TOPK = 3584, 1024, 8
 HLOC = 16
 UPW = 1024
-GROUP = 4
+GROUP = 2
+UP_TOK = 4
 OUT_CHUNK = 512
 
 DIMS = ((0, 1, 2), (1, 2, 0), (2, 0, 1))
-CHUNKS = ((0, 1152, 0), (1152, 1280, 1), (2432, 1152, 2))
+CHUNKS = (
+    (0, 640, 0), (640, 640, 1), (1280, 640, 2),
+    (1920, 512, 0), (2432, 640, 1), (3072, 512, 2),
+)
 STRIDE = (32, 1, 8)
 
 
@@ -39,14 +43,26 @@
 
 def coords(row_order, j):
     d1, d2, d3 = DIMS[j]
-    part = {d3: row_order // 64, d2: (row_order // 8) % 4, d1: (row_order // 2) % 4}
-    return part[0], part[1], part[2], (row_order // 32) % 2, row_order % 2
+    part = {d3: row_order >> 6, d2: (row_order >> 3) & 3, d1: (row_order >> 1) & 3}
+    return part[0], part[1], part[2], (row_order >> 5) & 1, row_order & 1
 
 
 def slot_index(x, y, z, c, s, j):
     pos = (x, y, z)
     d1, d2, d3 = DIMS[j]
-    return pos[d3] * 64 + c * 32 + pos[d2] * 8 + pos[d1] * 2 + s
+    return (pos[d3] << 6) + (c << 5) + (pos[d2] << 3) + (pos[d1] << 1) + s
+
+
+def hot(mask):
+    return jnp.where(mask, 1.0, 0.0).astype(BF16)
+
+
+def col_iota(n):
+    return iota((1, n), 1)
+
+
+def row_iota(n):
+    return iota((n, 1), 0)
 
 
 def layer_kernel(*refs):
@@ -58,9 +74,9 @@
 
     (lens, hid_h, ql_h, qr_h, cl_h, cr_h, vu_h, op_h, ng_h, eg_h, ed_h, ids_h, aff_h) = take(13)
     (out,) = take(1)
-    (hid, ql, qr, cl, cr, vu, op, ng, eg, ed, ids, aff) = take(12)
-    (ls, lr, ph, ps, pr, hb, hacc) = take(7)
-    (mt1, mt2, sel, whi, wlo) = take(5)
+    (hid, ql, qr, pairs, cl, cr, vu, op, ng, eg, ed, ids, aff) = take(13)
+    (ls, lr, ps, pr, hb, hacc) = take(6)
+    (mt1, mt2, sel, whi, wlo, order_in, order_out) = take(7)
     gat = take(n_chunk)
     sx = take(n_chunk)
     ox = take(n_chunk)
@@ -100,19 +116,20 @@
         return copy
 
     groups = TOK // GROUP
-    att_loads = []
+    qr_load = load(qr_h, qr, 2)
     small = [load(ids_h, ids, 0), load(aff_h, aff, 1)]
+
+    def att_copies(g):
+        sl = pl.ds(g * GROUP, GROUP)
+        return [
+            pltpu.make_async_copy(src.at[sl], dst.at[sl], ld.at[3 + 3 * g + n])
+            for n, (src, dst) in enumerate(((ql_h, ql), (cl_h, cl), (cr_h, cr)))
+        ]
+
     for g in range(groups):
-        sl = pl.ds(g * GROUP, GROUP)
-        att_loads.append(
-            [
-                load(ql_h.at[sl], ql.at[sl], 2 + 4 * g),
-                load(cl_h.at[sl], cl.at[sl], 3 + 4 * g),
-                load(qr_h.at[sl], qr.at[sl], 4 + 4 * g),
-                load(cr_h.at[sl], cr.at[sl], 5 + 4 * g),
-            ]
-        )
-    base = 2 + 4 * groups
+        for copy in att_copies(g):
+            copy.start()
+    base = 3 + 3 * groups
     vu_load = load(vu_h, vu, base)
     op_load = load(op_h, op, base + 1)
     hid_load = load(hid_h, hid, base + 2)
@@ -124,24 +141,22 @@
         copy.wait()
     ids_f = ids[...].astype(F32)
     affinity = aff[...]
-    weight = route_scale * affinity / jnp.sum(affinity, axis=1, keepdims=True)
+    weight = route_scale * affinity / jnp.sum(affinity, axis=0, keepdims=True)
     w_hi = weight.astype(BF16)
     w_lo = (weight - w_hi.astype(F32)).astype(BF16)
-    spread = (iota((TOPK, 128), 1) % TOPK == iota((TOPK, 128), 0)).astype(F32).astype(BF16)
-    own_lane = iota((TOK, 128), 1) // TOPK == iota((TOK, 128), 0)
+    spread = hot(col_iota(128) & 15 == row_iota(TOK))
+    own_lane = col_iota(128) >> 4 == row_iota(TOPK)
 
     def to_lanes(v):
         return jnp.sum(jnp.where(own_lane, dot(v, spread), 0.0), axis=0, keepdims=True)
 
     ids_b = ids_f.astype(BF16)
     id_row = to_lanes(ids_b)
-    rep = (iota((128, TOK), 0) // TOPK == iota((128, TOK), 1)).astype(F32).astype(BF16)
+    rep = hot(row_iota(128) >> 4 == col_iota(TOPK))
     id_col = jnp.sum(
-        jnp.where(iota((128, TOPK), 0) % TOPK == iota((128, TOPK), 1), dot(rep, ids_b), 0.0),
-        axis=1,
-        keepdims=True,
+        jnp.where(row_iota(128) & 15 == col_iota(TOK), dot(rep, ids_b), 0.0), axis=1, keepdims=True
     )
-    earlier = (id_col == id_row) & (iota((128, 128), 0) < iota((128, 128), 1))
+    earlier = (id_col == id_row) & (row_iota(128) < col_iota(128))
     slot_row = jnp.sum(jnp.where(earlier, 1.0, 0.0), axis=0, keepdims=True)
     mrow = iota((16, 128), 0)
     meta = jnp.where(
@@ -152,46 +167,53 @@
     for d in range(3):
         mt1[d, pos[d]] = meta
 
-    position = iota((HEADS, CTX), 1)
+    position = col_iota(CTX)
+    own_half = col_iota(2 * ROPE) >> 6 == row_iota(HEADS) & 1
+    pair_row = col_iota(HEADS // 2 * TOK) - ((row_iota(HEADS) >> 1) << 4)
+    qr_load.wait()
+    for n in range(HEADS // 2):
+        pairs[n] = qr[:, n * 2 * ROPE : (n + 1) * 2 * ROPE]
 
     def attend(t):
         q, kv = ql[t], cl[t]
-        scores = dot_nt(q, kv) + dot(qr[t], cr[t])
+        pick = hot(pair_row == t)
+        rot = dot(pick, pairs[...].reshape(HEADS // 2 * TOK, 2 * ROPE))
+        rot = jnp.where(own_half, rot, 0.0).astype(BF16)
+        scores = dot_nt(q, kv) + dot(rot, jnp.concatenate([cr[t], cr[t]], axis=0))
         scores = jnp.where(position < lens[t], scores * score_scale, -jnp.inf)
         raised = jnp.exp(scores - jnp.max(scores, axis=1, keepdims=True))
         probs = (raised / jnp.sum(raised, axis=1, keepdims=True)).astype(BF16)
         latent = dot(probs, kv).astype(BF16)
         for g in range(4):
             ls[g, t] = latent[g * HLOC : (g + 1) * HLOC]
-
-    lat_sends = []
-    for g in range(groups):
-        for copy in att_loads[g]:
+        lr[y, t] = ls[y, t]
+
+    def attend_group(g):
+        for copy in att_copies(g):
             copy.wait()
-
-        def step(i, carry):
-            for u in range(2):
-                attend(g * GROUP + i * 2 + u)
-            return carry
-
-        lax.fori_loop(0, GROUP // 2, step, 0)
-        if g == 0:
-            pl.semaphore_wait(barrier, len(peers))
+        for u in range(GROUP):
+            attend(g * GROUP + u)
+
+    def lat_copy(g, k):
+        to = at(1, k)
+        sl = pl.ds(g * GROUP, GROUP)
+        return remote(ls.at[to[1], sl], lr.at[y, sl], lat_s.at[g, k], lat_r.at[g, k], to)
+
+    attend_group(0)
+    pl.semaphore_wait(barrier, len(peers))
+    for k in (2, 1, 3):
+        lat_copy(0, k).start()
+    for d in range(3):
+        for k in (1, 2, 3):
+            remote(mt1.at[d, pos[d]], mt1.at[d, pos[d]], m1_s.at[d], m1_r.at[d], at(d, k)).start()
+
+    def attend_step(g, carry):
+        attend_group(g)
         for k in (2, 1, 3):
-            to = at(1, k)
-            copy = remote(
-                ls.at[to[1], pl.ds(g * GROUP, GROUP)],
-                lr.at[y, pl.ds(g * GROUP, GROUP)],
-                lat_s.at[g, k],
-                lat_r.at[g, k],
-                to,
-            )
-            copy.start()
-            lat_sends.append(copy)
-        if g == 0:
-            for d in range(3):
-                for k in (1, 2, 3):
-                    remote(mt1.at[d, pos[d]], mt1.at[d, pos[d]], m1_s.at[d], m1_r.at[d], at(d, k)).start()
+            lat_copy(g, k).start()
+        return carry
+
+    lax.fori_loop(1, groups, attend_step, 0)
 
     for j in range(3):
         d1, d2, _ = DIMS[j]
@@ -203,49 +225,22 @@
             remote(mt2.at[j, pos[d2]], mt2.at[j, pos[d2]], m2_s.at[j], m2_r.at[j], at(d2, k)).start()
 
     vu_load.wait()
-    diag = iota((TOK * HLOC, UPW), 0) % HLOC == iota((TOK * HLOC, UPW), 1) // 64
-    fold = (iota((TOK, TOK * HLOC), 1) // HLOC == iota((TOK, TOK * HLOC), 0)).astype(F32).astype(BF16)
-
-    def up(latents, src):
-        wide = dot(latents.reshape(TOK * HLOC, LAT), vu[...])
-        ph[src] = dot(fold, jnp.where(diag, wide, 0.0).astype(BF16)).astype(BF16)
-
-    up(ls[y], y)
-
-    row = iota((256, 128), 0)
-    pick_row = iota((256, 256), 0)
-    pick_col = iota((256, 256), 1)
-    tok_of_lane = (iota((128, 256), 0) // TOPK == iota((128, 256), 1) % TOK).astype(F32).astype(BF16)
-    tok_of_lane_t = (iota((256, 128), 1) // TOPK == iota((256, 128), 0) % TOK).astype(F32).astype(BF16)
-    for j in range(3):
-        _, _, d3 = DIMS[j]
-        remote(mt2.at[j, pl.ds(0, 3)], mt2.at[j, pl.ds(0, 3)], m2_s.at[j], m2_r.at[j], me).wait_recv()
-        facts = mt2[j].reshape(256, 128)
-
-        def of_source(n):
-            hot = pick_col == ((pick_row // 2) % 16) * 16 + n
-            return dot(hot.astype(F32).astype(BF16), facts)
-
-        here = sum(pos[d] * STRIDE[d] for d in range(3) if d != d3)
-        expert = here + (row // 64) * STRIDE[d3] + ((row // 32) % 2) * 4
-        match = (of_source(0) == expert.astype(F32)) & (of_source(1) == (row % 2).astype(F32))
-        same = (pick_row // 2) % 16 == pick_col // TOK
-        hit = jnp.where(match, 1.0, 0.0).astype(BF16)
-        sel[j] = jnp.where(same, dot(hit, tok_of_lane), 0.0).astype(BF16)
-        same_t = (pick_col // 2) % 16 == pick_row // TOK
-        for n, ref in ((2, whi), (3, wlo)):
-            val = jnp.where(match, of_source(n), 0.0).astype(BF16)
-            ref[j] = jnp.where(same_t, dot_nt(tok_of_lane_t, val), 0.0).astype(BF16)
-
-    for k in (1, 3, 2):
-        for g in range(groups):
-            sl = pl.ds(g * GROUP, GROUP)
-            remote(ls.at[0, sl], lr.at[0, sl], lat_s.at[g, k], lat_r.at[g, k], me).wait_recv()
-        src = (y + 4 - k) % 4
-        up(lr[src], src)
+    up_rows = 4 * UP_TOK * HLOC
+    diag = row_iota(up_rows) & (HLOC - 1) == col_iota(UPW) >> 6
+    from_row = row_iota(4 * TOK)
+    from_col = col_iota(up_rows)
+    heads_out = jnp.zeros((4 * TOK, UPW), F32)
+    for u in range(TOK // UP_TOK):
+        for g in range(u * UP_TOK // GROUP, (u + 1) * UP_TOK // GROUP):
+            for k in (1, 3, 2):
+                lat_copy(g, k).wait_recv()
+        latents = lr[:, pl.ds(u * UP_TOK, UP_TOK)].reshape(up_rows, LAT)
+        wide = jnp.where(diag, dot(latents, vu[...]), 0.0).astype(BF16)
+        fold = hot(((from_col >> 6) << 4) + u * UP_TOK + ((from_col >> 4) & 3) == from_row)
+        heads_out = heads_out + dot(fold, wide)
+    heads_out = heads_out.astype(BF16)
 
     op_load.wait()
-    heads_out = ph[...].reshape(4 * TOK, UPW)
 
     def project(n, carry):
         cols = pl.ds(pl.multiple_of(n * OUT_CHUNK, OUT_CHUNK), OUT_CHUNK)
@@ -257,6 +252,45 @@
         return carry
 
     lax.fori_loop(0, D // OUT_CHUNK, project, 0)
+    row = row_iota(256)
+    col = col_iota(256)
+    source = (row >> 1) & 15
+    expand = hot(source == col_iota(16))
+    gather_fact = hot(((row_iota(64) & 15) << 4) + (row_iota(64) >> 4) == col)
+
+    def facts_of(j):
+        d3 = DIMS[j][2]
+        packed = dot(gather_fact, mt2[j].reshape(256, 128)).astype(BF16)
+        here = sum(pos[d] * STRIDE[d] for d in range(3) if d != d3)
+        expert = here + (row >> 6) * STRIDE[d3] + ((row >> 5) & 1) * 4
+        ident, slot = dot(expand, packed[0:16]), dot(expand, packed[16:32])
+        match = (ident == expert.astype(F32)) & (slot == (row & 1).astype(F32))
+        return packed, match
+
+    def build_select(j):
+        tok_of_lane = hot(row_iota(128) & 15 == col & 15)
+        match = facts_of(j)[1]
+        sel[j] = jnp.where(source == col >> 4, dot(hot(match), tok_of_lane), 0.0).astype(BF16)
+
+    def build_weights(j):
+        lane_token = hot(col_iota(128) & 15 == row & 15)
+        packed, match = facts_of(j)
+        for n, ref in ((2, whi), (3, wlo)):
+            val = jnp.where(match, dot(expand, packed[16 * n : 16 * n + 16]), 0.0).astype(BF16)
+            spread_out = dot_nt(lane_token, val)
+            ref[j] = jnp.where((col >> 1) & 15 == row >> 4, spread_out, 0.0).astype(BF16)
+
+    def build_order(j):
+        order_in[j - 1] = hot(slot_index(*coords(row, 0), j) == col)
+        order_out[j - 1] = hot(slot_index(*coords(row, j), 0) == col)
+
+    for j in range(3):
+        remote(mt2.at[j, pl.ds(0, 3)], mt2.at[j, pl.ds(0, 3)], m2_s.at[j], m2_r.at[j], me).wait_recv()
+    for j in range(3):
+        build_select(j)
+    for j in (1, 2):
+        build_order(j)
+
     hid_load.wait()
     ng_load.wait()
     pr[y] = ps[y]
@@ -268,7 +302,7 @@
     hid[...] = hidden
     wide = hidden.astype(F32)
     inv = lax.rsqrt(jnp.mean(wide * wide, axis=1, keepdims=True) + norm_eps)
-    normed = (wide * inv * ng[...]).astype(BF16)
+    normed = (wide * inv * ng[...].reshape(1, D)).astype(BF16)
 
     def exchange(ph_no, i, src, dst, to):
         remote(src, dst, ex_s.at[ph_no, i], ex_r.at[ph_no, i], to).start()
@@ -304,16 +338,15 @@
         sx[i][...] = rows.reshape(8, 32, n)
         to_line(2, i, d3, sx[i], ox[i])
 
-    def reorder(to_j, from_j):
-        want = slot_index(*coords(pick_row, to_j), from_j)
-        return (want == pick_col).astype(F32).astype(BF16)
+    for j in range(3):
+        build_weights(j)
 
     eg_load.wait()
     for i, (lo, n, j) in enumerate(CHUNKS):
         arrived(2, i, ox[i], 7)
         rows = ox[i][...].reshape(256, n)
         if j != 0:
-            rows = dot(reorder(0, j), rows).astype(BF16)
+            rows = dot(order_in[j - 1], rows).astype(BF16)
         part = dot(rows, eg[lo : lo + n, :])
         if i == 0:
             hacc[...] = part
@@ -321,15 +354,14 @@
             hacc[...] += part
         else:
             v = hacc[...] + part
-            hb[...] = (v / (1.0 + jnp.exp(-v))).astype(BF16)
+            hb[0] = (v / (1.0 + jnp.exp(-v))).astype(BF16)
     ed_load.wait()
     for i, (lo, n, j) in enumerate(CHUNKS):
-        d1, d2, d3 = DIMS[j]
-        rows = dot(hb[...], ed[:, lo : lo + n]).astype(BF16)
-        if j != 0:
-            rows = dot(reorder(j, 0), rows).astype(BF16)
+        if i in (1, 2):
+            hb[j] = dot(order_out[j - 1], hb[0]).astype(BF16)
+        rows = dot(hb[j], ed[:, lo : lo + n]).astype(BF16)
         yx[i][...] = rows.reshape(8, 32, n)
-        to_line(3, i, d3, yx[i], qx[i])
+        to_line(3, i, DIMS[j][2], yx[i], qx[i])
 
     for i, (lo, n, j) in enumerate(CHUNKS):
         d1, d2, d3 = DIMS[j]
@@ -357,8 +389,9 @@
             acc = acc + vx[i][q].astype(F32)
         out[:, lo : lo + n] = acc.astype(BF16)
 
-    for copy in lat_sends:
-        copy.wait_send()
+    for g in range(groups):
+        for k in (1, 2, 3):
+            lat_copy(g, k).wait_send()
     remote(ps.at[pl.ds(0, 3)], pr.at[pl.ds(0, 3)], rs_s, rs_r, me).wait_send()
     for d in range(3):
         remote(mt1.at[d, pl.ds(0, 3)], mt1.at[d, pl.ds(0, 3)], m1_s.at[d], m1_r.at[d], me).wait_send()
@@ -397,33 +430,35 @@
     scratch = [
         v((TOK, D), BF16),
         v((TOK, HEADS, LAT), BF16),
-        v((TOK, HEADS, ROPE), BF16),
+        v((TOK, HEADS * ROPE), BF16),
+        v((HEADS // 2, TOK, 2 * ROPE), BF16),
         v((TOK, CTX, LAT), BF16),
         v((TOK, ROPE, CTX), BF16),
         v((LAT, UPW), BF16),
         v((UPW, D), BF16),
-        v((1, D), F32),
+        v((D,), F32),
         v((D, FF), BF16),
         v((FF, D), BF16),
-        v((TOK, TOPK), jnp.int32),
-        v((TOK, TOPK), F32),
+        v((TOPK, TOK), jnp.int32),
+        v((TOPK, TOK), F32),
         v((4, TOK, HLOC, LAT), BF16),
         v((4, TOK, HLOC, LAT), BF16),
-        v((4, TOK, UPW), BF16),
         v((4, TOK, D), BF16),
         v((4, TOK, D), BF16),
-        v((256, FF), BF16),
+        v((3, 256, FF), BF16),
         v((256, FF), F32),
         v((3, 4, 16, 128), BF16),
         v((3, 4, 4, 16, 128), BF16),
         v((3, 256, 256), BF16),
         v((3, 256, 256), BF16),
         v((3, 256, 256), BF16),
+        v((2, 256, 256), BF16),
+        v((2, 256, 256), BF16),
     ]
     for shape in ((4, 4, TOK), (8, 32), (8, 32), (8, 32), (8, 32), (4, 64), (4, 64), (4, TOK), (4, TOK)):
         scratch += [v(shape + (n,), BF16) for _, n, _ in CHUNKS]
     scratch += [
-        dma((2 + TOK + 6,)),
+        dma((3 + 3 * (TOK // GROUP) + 6,)),
         dma((TOK // GROUP, 4)),
         dma((TOK // GROUP, 4)),
         dma,
@@ -450,16 +485,16 @@
         lengths,
         hidden_in,
         query_latent,
-        query_rope.reshape(TOK, HEADS, ROPE),
+        query_rope,
         cache_latent,
         cache_rope,
         value_up,
         out_proj,
-        norm_gain.reshape(1, D),
+        norm_gain,
         expert_gate,
         expert_down,
-        expert_ids,
-        affinity,
+        expert_ids.T,
+        affinity.T,
     )
 
 

time: 91 us -> 75.6 us (0.83)
  Pallas kernels: 83.1 us -> 73.9 us
  local copies, waits for them, and re-layouts: 7.46 us -> 1.55 us
    pallas_call x1, Pallas kernels: 83.1 us -> 73.9 us  [per_device(): pl.pallas_call(layer_kernel, out_shape=jax.ShapeDtypeStruct((TOK, D), BF1...]
    reshape x2 -> x0, local copies, waits for them, and re-layouts: 3.21 us -> none  [the longest x1 1.88 us: per_device(): query_rope.reshape(TOK, HEADS, ROPE)]
    unnamed x3 -> x1, local copies, waits for them, and re-layouts: 4.26 us -> 1.55 us
where the time goes in v2:
time: 75.6 us; the launch traced here: 75.4 us
  Pallas kernels  73.9 us (98%)
  local copies, waits for them, and re-layouts  1.55 us (2%)
    pallas_call x1, Pallas kernels, per_device(): pl.pallas_call(layer_kernel, out_shape=jax.ShapeDtypeStruct((TOK, D), BF1...  73.9 us
    unnamed x1, local copies, waits for them, and re-layouts  1.55 us

profile of v2, /device:TPU:1, one launch (start us, length us, event | category | flops | bytes accessed | tf_op | source)
XLA Modules:
  0.0 75.4 jit_solution(292441635827250966)
XLA Ops:
  0.0 73.9 %layer.1 = bf16[16,3584]{1,0:T(8,128)(2,1)} custom-call(s32[16]{0:T(128)} %refs_0_.1, bf16[16,3584]{1,0:T(8,128)(2,1)} %refs_1_.1, bf16[16,64,512]{2,1,0:T(8,128)(2,1)} %refs_2_.1, bf16[16,4096]{1,0:T(8,128)(2,1)} %refs_3_.1, bf16[16,128,512]{2,1,0:T(8,128)(2,1)} %refs_4_.1, bf16[16,64,128]{2,1,0:T(8,128)(2,1)} %refs_5_.1, bf16[512,1024]{1,0:T(8,128)(2,1)} %refs_6_.1, ...), custom_call_target="tpu_custom_call" | custom-call | tf_op jit(solution)/shard_map/layer/pallas_call | solution.py:474
  73.9 1.6 %copy.15 = bf16[16,3584]{1,0:T(8,128)(2,1)} copy(bf16[16,3584]{1,0:T(8,128)(2,1)} %layer.1) | data formatting | bytes 229376

commit v3 on v2

--- a/solution.py
+++ b/solution.py
@@ -19,13 +19,11 @@
 UPW = 1024
 GROUP = 2
 UP_TOK = 4
-OUT_CHUNK = 512
 
 DIMS = ((0, 1, 2), (1, 2, 0), (2, 0, 1))
-CHUNKS = (
-    (0, 640, 0), (640, 640, 1), (1280, 640, 2),
-    (1920, 512, 0), (2432, 640, 1), (3072, 512, 2),
-)
+CHUNKS = ((0, 512, 2), (512, 512, 0), (1024, 512, 1), (1536, 384, 2), (1920, 384, 0), (2304, 384, 1), (2688, 256, 2), (2944, 384, 0), (3328, 256, 1))
+WIDTHS = tuple(n for _, n, _ in CHUNKS[:-1]) + (CHUNKS[-1][1] + 128,)
+BACK = ((0, 512, 2), (512, 512, 0), (1024, 512, 1), (1536, 384, 2), (1920, 384, 0), (2304, 384, 1), (2688, 256, 2), (2944, 384, 0), (3328, 256, 1))
 STRIDE = (32, 1, 8)
 
 
@@ -67,6 +65,7 @@
 
 def layer_kernel(*refs):
     n_chunk = len(CHUNKS)
+    n_back = len(BACK)
     it = iter(refs)
 
     def take(n):
@@ -80,12 +79,12 @@
     gat = take(n_chunk)
     sx = take(n_chunk)
     ox = take(n_chunk)
-    yx = take(n_chunk)
-    qx = take(n_chunk)
-    px = take(n_chunk)
-    ux = take(n_chunk)
-    tx = take(n_chunk)
-    vx = take(n_chunk)
+    yx = take(n_back)
+    qx = take(n_back)
+    px = take(n_back)
+    ux = take(n_back)
+    tx = take(n_back)
+    vx = take(n_back)
     (ld, lat_s, lat_r, rs_s, rs_r, m1_s, m1_r, m2_s, m2_r, ex_s, ex_r) = take(11)
 
     dp = lax.axis_index("dp")
@@ -137,6 +136,42 @@
     eg_load = load(eg_h.at[0], eg, base + 4)
     ed_load = load(ed_h.at[0], ed, base + 5)
 
+    position = col_iota(CTX)
+    own_half = col_iota(2 * ROPE) >> 6 == row_iota(HEADS) & 1
+    pair_row = col_iota(HEADS // 2 * TOK) - ((row_iota(HEADS) >> 1) << 4)
+    qr_load.wait()
+    for n in range(HEADS // 2):
+        pairs[n] = qr[:, n * 2 * ROPE : (n + 1) * 2 * ROPE]
+
+    def attend(t):
+        q, kv = ql[t], cl[t]
+        pick = hot(pair_row == t)
+        rot = dot(pick, pairs[...].reshape(HEADS // 2 * TOK, 2 * ROPE))
+        rot = jnp.where(own_half, rot, 0.0).astype(BF16)
+        scores = dot_nt(q, kv) + dot(rot, jnp.concatenate([cr[t], cr[t]], axis=0))
+        scores = jnp.where(position < lens[t], scores * score_scale, -jnp.inf)
+        raised = jnp.exp(scores - jnp.max(scores, axis=1, keepdims=True))
+        probs = (raised / jnp.sum(raised, axis=1, keepdims=True)).astype(BF16)
+        latent = dot(probs, kv).astype(BF16)
+        for g in range(4):
+            ls[g, t] = latent[g * HLOC : (g + 1) * HLOC]
+        lr[y, t] = ls[y, t]
+
+    def attend_group(g):
+        for copy in att_copies(g):
+            copy.wait()
+        for u in range(GROUP):
+            attend(g * GROUP + u)
+
+    def lat_copy(g, k):
+        to = at(1, k)
+        sl = pl.ds(g * GROUP, GROUP)
+        return remote(ls.at[to[1], sl], lr.at[y, sl], lat_s.at[g, k], lat_r.at[g, k], to)
+
+    attend_group(0)
+    pl.semaphore_wait(barrier, len(peers))
+    for k in (2, 1, 3):
+        lat_copy(0, k).start()
     for copy in small:
         copy.wait()
     ids_f = ids[...].astype(F32)
@@ -167,42 +202,6 @@
     for d in range(3):
         mt1[d, pos[d]] = meta
 
-    position = col_iota(CTX)
-    own_half = col_iota(2 * ROPE) >> 6 == row_iota(HEADS) & 1
-    pair_row = col_iota(HEADS // 2 * TOK) - ((row_iota(HEADS) >> 1) << 4)
-    qr_load.wait()
-    for n in range(HEADS // 2):
-        pairs[n] = qr[:, n * 2 * ROPE : (n + 1) * 2 * ROPE]
-
-    def attend(t):
-        q, kv = ql[t], cl[t]
-        pick = hot(pair_row == t)
-        rot = dot(pick, pairs[...].reshape(HEADS // 2 * TOK, 2 * ROPE))
-        rot = jnp.where(own_half, rot, 0.0).astype(BF16)
-        scores = dot_nt(q, kv) + dot(rot, jnp.concatenate([cr[t], cr[t]], axis=0))
-        scores = jnp.where(position < lens[t], scores * score_scale, -jnp.inf)
-        raised = jnp.exp(scores - jnp.max(scores, axis=1, keepdims=True))
-        probs = (raised / jnp.sum(raised, axis=1, keepdims=True)).astype(BF16)
-        latent = dot(probs, kv).astype(BF16)
-        for g in range(4):
-            ls[g, t] = latent[g * HLOC : (g + 1) * HLOC]
-        lr[y, t] = ls[y, t]
-
-    def attend_group(g):
-        for copy in att_copies(g):
-            copy.wait()
-        for u in range(GROUP):
-            attend(g * GROUP + u)
-
-    def lat_copy(g, k):
-        to = at(1, k)
-        sl = pl.ds(g * GROUP, GROUP)
-        return remote(ls.at[to[1], sl], lr.at[y, sl], lat_s.at[g, k], lat_r.at[g, k], to)
-
-    attend_group(0)
-    pl.semaphore_wait(barrier, len(peers))
-    for k in (2, 1, 3):
-        lat_copy(0, k).start()
     for d in range(3):
         for k in (1, 2, 3):
             remote(mt1.at[d, pos[d]], mt1.at[d, pos[d]], m1_s.at[d], m1_r.at[d], at(d, k)).start()
@@ -241,17 +240,58 @@
     heads_out = heads_out.astype(BF16)
 
     op_load.wait()
-
-    def project(n, carry):
-        cols = pl.ds(pl.multiple_of(n * OUT_CHUNK, OUT_CHUNK), OUT_CHUNK)
-        part = dot(heads_out, op[:, cols]).astype(BF16)
-        ps[:, :, cols] = part.reshape(4, TOK, OUT_CHUNK)
+    for i, (lo, n, j) in enumerate(CHUNKS):
+        part = dot(heads_out, op[:, lo : lo + n]).astype(BF16)
+        ps[:, :, lo : lo + n] = part.reshape(4, TOK, n)
         for k in (2, 1, 3):
             to = at(1, k)
-            remote(ps.at[to[1], :, cols], pr.at[y, :, cols], rs_s, rs_r, to).start()
-        return carry
-
-    lax.fori_loop(0, D // OUT_CHUNK, project, 0)
+            cols = pl.ds(lo, n)
+            remote(ps.at[to[1], :, cols], pr.at[y, :, cols], rs_s.at[i], rs_r.at[i], to).start()
+
+    def exchange(ph_no, i, src, dst, to):
+        remote(src, dst, ex_s.at[ph_no, i], ex_r.at[ph_no, i], to).start()
+
+    def arrived(ph_no, i, ref, n):
+        remote(ref.at[pl.ds(0, n)], ref.at[pl.ds(0, n)], ex_s.at[ph_no, i], ex_r.at[ph_no, i], me).wait_recv()
+
+    line = [(k, dc) for k in (2, 1, 3, 0) for dc in (0, 1) if (k, dc) != (0, 0)]
+
+    def to_line(ph_no, i, d3, src, dst):
+        slot = pos[d3] * 2 + c
+        for k, dc in line:
+            there = ((pos[d3] + k) % 4) * 2 + (c + dc) % 2
+            exchange(ph_no, i, src.at[there], dst.at[slot], at(d3, k, dc))
+        dst[slot] = src[slot]
+
+    hid_load.wait()
+    ng_load.wait()
+    gain = ng[...].reshape(1, D)
+    pr[y] = ps[y]
+    squares = jnp.zeros((TOK, 1), F32)
+    for i, (lo, n, j) in enumerate(CHUNKS):
+        d1, d2, d3 = DIMS[j]
+        cols = pl.ds(lo, n)
+        got = pr.at[pl.ds(0, 3), :, cols]
+        remote(got, got, rs_s.at[i], rs_r.at[i], me).wait_recv()
+        total = hid[:, lo : lo + n].astype(F32)
+        for src in range(4):
+            total = total + pr[src, :, lo : lo + n].astype(F32)
+        hidden = total.astype(BF16)
+        hid[:, lo : lo + n] = hidden
+        wide = hidden.astype(F32)
+        squares = squares + jnp.sum(wide * wide, axis=1, keepdims=True)
+        scaled = (wide * gain[:, lo : lo + n]).astype(BF16)
+        if i == n_chunk - 1:
+            inv = lax.rsqrt(squares / D + norm_eps)
+            inv_hi = inv.astype(BF16).astype(F32)
+            lane = col_iota(128)
+            extra = jnp.where(lane == 0, inv_hi, jnp.where(lane == 1, inv - inv_hi, 0.0))
+            scaled = jnp.concatenate([scaled, extra.astype(BF16)], axis=1)
+        gat[i][pos[d2], pos[d1]] = scaled
+        for k in (2, 1, 3):
+            mine = gat[i].at[pos[d2], pos[d1]]
+            exchange(0, i, mine, mine, at(d1, k))
+
     row = row_iota(256)
     col = col_iota(256)
     source = (row >> 1) & 15
@@ -291,40 +331,6 @@
     for j in (1, 2):
         build_order(j)
 
-    hid_load.wait()
-    ng_load.wait()
-    pr[y] = ps[y]
-    remote(ps.at[pl.ds(0, 3)], pr.at[pl.ds(0, 3)], rs_s, rs_r, me).wait_recv()
-    total = hid[...].astype(F32)
-    for src in range(4):
-        total = total + pr[src].astype(F32)
-    hidden = total.astype(BF16)
-    hid[...] = hidden
-    wide = hidden.astype(F32)
-    inv = lax.rsqrt(jnp.mean(wide * wide, axis=1, keepdims=True) + norm_eps)
-    normed = (wide * inv * ng[...].reshape(1, D)).astype(BF16)
-
-    def exchange(ph_no, i, src, dst, to):
-        remote(src, dst, ex_s.at[ph_no, i], ex_r.at[ph_no, i], to).start()
-
-    def arrived(ph_no, i, ref, n):
-        remote(ref.at[pl.ds(0, n)], ref.at[pl.ds(0, n)], ex_s.at[ph_no, i], ex_r.at[ph_no, i], me).wait_recv()
-
-    line = [(k, dc) for k in (2, 1, 3, 0) for dc in (0, 1) if (k, dc) != (0, 0)]
-
-    def to_line(ph_no, i, d3, src, dst):
-        slot = pos[d3] * 2 + c
-        for k, dc in line:
-            there = ((pos[d3] + k) % 4) * 2 + (c + dc) % 2
-            exchange(ph_no, i, src.at[there], dst.at[slot], at(d3, k, dc))
-        dst[slot] = src[slot]
-
-    for i, (lo, n, j) in enumerate(CHUNKS):
-        d1, d2, d3 = DIMS[j]
-        gat[i][pos[d2], pos[d1]] = normed[:, lo : lo + n]
-        for k in (2, 1, 3):
-            mine = gat[i].at[pos[d2], pos[d1]]
-            exchange(0, i, mine, mine, at(d1, k))
     for i, (lo, n, j) in enumerate(CHUNKS):
         d1, d2, d3 = DIMS[j]
         arrived(0, i, gat[i].at[0], 3)
@@ -334,8 +340,8 @@
     for i, (lo, n, j) in enumerate(CHUNKS):
         d1, d2, d3 = DIMS[j]
         arrived(1, i, gat[i], 3)
-        rows = dot(sel[j], gat[i][...].reshape(256, n)).astype(BF16)
-        sx[i][...] = rows.reshape(8, 32, n)
+        rows = dot(sel[j], gat[i][...].reshape(256, WIDTHS[i])).astype(BF16)
+        sx[i][...] = rows.reshape(8, 32, WIDTHS[i])
         to_line(2, i, d3, sx[i], ox[i])
 
     for j in range(3):
@@ -344,26 +350,27 @@
     eg_load.wait()
     for i, (lo, n, j) in enumerate(CHUNKS):
         arrived(2, i, ox[i], 7)
-        rows = ox[i][...].reshape(256, n)
+        rows = ox[i][...].reshape(256, WIDTHS[i])
         if j != 0:
             rows = dot(order_in[j - 1], rows).astype(BF16)
-        part = dot(rows, eg[lo : lo + n, :])
+        part = dot(rows[:, :n], eg[lo : lo + n, :])
         if i == 0:
             hacc[...] = part
         elif i < n_chunk - 1:
             hacc[...] += part
         else:
-            v = hacc[...] + part
+            inv = rows[:, n : n + 1].astype(F32) + rows[:, n + 1 : n + 2].astype(F32)
+            v = (hacc[...] + part) * inv
             hb[0] = (v / (1.0 + jnp.exp(-v))).astype(BF16)
     ed_load.wait()
-    for i, (lo, n, j) in enumerate(CHUNKS):
-        if i in (1, 2):
+    for i, (lo, n, j) in enumerate(BACK):
+        if i < 3 and j != 0:
             hb[j] = dot(order_out[j - 1], hb[0]).astype(BF16)
         rows = dot(hb[j], ed[:, lo : lo + n]).astype(BF16)
         yx[i][...] = rows.reshape(8, 32, n)
         to_line(3, i, DIMS[j][2], yx[i], qx[i])
 
-    for i, (lo, n, j) in enumerate(CHUNKS):
+    for i, (lo, n, j) in enumerate(BACK):
         d1, d2, d3 = DIMS[j]
         arrived(3, i, qx[i], 7)
         rows = qx[i][...].reshape(256, n)
@@ -372,7 +379,7 @@
         for k in (2, 1, 3):
             exchange(4, i, px[i].at[(pos[d2] + k) % 4], ux[i].at[pos[d2]], at(d2, k))
         ux[i][pos[d2]] = px[i][pos[d2]]
-    for i, (lo, n, j) in enumerate(CHUNKS):
+    for i, (lo, n, j) in enumerate(BACK):
         d1, d2, d3 = DIMS[j]
         arrived(4, i, ux[i], 3)
         acc = ux[i][0].astype(F32)
@@ -382,7 +389,7 @@
         for k in (2, 1, 3):
             exchange(5, i, tx[i].at[(pos[d1] + k) % 4], vx[i].at[pos[d1]], at(d1, k))
         vx[i][pos[d1]] = tx[i][pos[d1]]
-    for i, (lo, n, j) in enumerate(CHUNKS):
+    for i, (lo, n, j) in enumerate(BACK):
         arrived(5, i, vx[i], 3)
         acc = hid[:, lo : lo + n].astype(F32)
         for q in range(4):
@@ -392,21 +399,24 @@
     for g in range(groups):
         for k in (1, 2, 3):
             lat_copy(g, k).wait_send()
-    remote(ps.at[pl.ds(0, 3)], pr.at[pl.ds(0, 3)], rs_s, rs_r, me).wait_send()
+    for i, (lo, n, j) in enumerate(CHUNKS):
+        left = ps.at[pl.ds(0, 3), :, pl.ds(lo, n)]
+        remote(left, left, rs_s.at[i], rs_r.at[i], me).wait_send()
     for d in range(3):
         remote(mt1.at[d, pl.ds(0, 3)], mt1.at[d, pl.ds(0, 3)], m1_s.at[d], m1_r.at[d], me).wait_send()
         remote(mt2.at[d, pl.ds(0, 3)], mt2.at[d, pl.ds(0, 3)], m2_s.at[d], m2_r.at[d], me).wait_send()
+    def left(ph_no, i, ref, n):
+        part = ref.at[pl.ds(0, n)]
+        remote(part, part, ex_s.at[ph_no, i], ex_r.at[ph_no, i], me).wait_send()
+
     for i in range(n_chunk):
-        for ph_no, ref, n in (
-            (0, gat[i].at[0], 3),
-            (1, gat[i], 3),
-            (2, sx[i], 7),
-            (3, yx[i], 7),
-            (4, px[i], 3),
-            (5, tx[i], 3),
-        ):
-            part = ref.at[pl.ds(0, n)]
-            remote(part, part, ex_s.at[ph_no, i], ex_r.at[ph_no, i], me).wait_send()
+        left(0, i, gat[i].at[0], 3)
+        left(1, i, gat[i], 3)
+        left(2, i, sx[i], 7)
+    for i in range(n_back):
+        left(3, i, yx[i], 7)
+        left(4, i, px[i], 3)
+        left(5, i, tx[i], 3)
 
 
 def per_device(
@@ -425,6 +435,7 @@
     affinity,
 ):
     n_chunk = len(CHUNKS)
+    n_back = len(BACK)
     dma = pltpu.SemaphoreType.DMA
     v = pltpu.VMEM
     scratch = [
@@ -455,20 +466,22 @@
         v((2, 256, 256), BF16),
         v((2, 256, 256), BF16),
     ]
-    for shape in ((4, 4, TOK), (8, 32), (8, 32), (8, 32), (8, 32), (4, 64), (4, 64), (4, TOK), (4, TOK)):
-        scratch += [v(shape + (n,), BF16) for _, n, _ in CHUNKS]
+    for shape in ((4, 4, TOK), (8, 32), (8, 32)):
+        scratch += [v(shape + (n,), BF16) for n in WIDTHS]
+    for shape in ((8, 32), (8, 32), (4, 64), (4, 64), (4, TOK), (4, TOK)):
+        scratch += [v(shape + (n,), BF16) for _, n, _ in BACK]
     scratch += [
         dma((3 + 3 * (TOK // GROUP) + 6,)),
         dma((TOK // GROUP, 4)),
         dma((TOK // GROUP, 4)),
-        dma,
-        dma,
+        dma((n_chunk,)),
+        dma((n_chunk,)),
         dma((3,)),
         dma((3,)),
         dma((3,)),
         dma((3,)),
-        dma((6, n_chunk)),
-        dma((6, n_chunk)),
+        dma((6, max(n_chunk, n_back))),
+        dma((6, max(n_chunk, n_back))),
     ]
     anyspace = pl.BlockSpec(memory_space=pl.ANY)
     return pl.pallas_call(

time: 75.6 us -> 73.1 us (0.967)
  Pallas kernels: 73.9 us -> 71.5 us
    pallas_call x1, Pallas kernels: 73.9 us -> 71.5 us  [per_device(): pl.pallas_call(layer_kernel, out_shape=jax.ShapeDtypeStruct((TOK, D), BF1...]
where the time goes in v3:
time: 73.1 us; the launch traced here: 73 us
  Pallas kernels  71.5 us (98%)
  local copies, waits for them, and re-layouts  1.55 us (2%)
    pallas_call x1, Pallas kernels, per_device(): pl.pallas_call(layer_kernel, out_shape=jax.ShapeDtypeStruct((TOK, D), BF1...  71.5 us
    unnamed x1, local copies, waits for them, and re-layouts  1.55 us

profile of v3, /device:TPU:1, one launch (start us, length us, event | category | flops | bytes accessed | tf_op | source)
XLA Modules:
  0.0 73.0 jit_solution(1035627172047115153)
XLA Ops:
  0.0 71.5 %layer.1 = bf16[16,3584]{1,0:T(8,128)(2,1)} custom-call(s32[16]{0:T(128)} %refs_0_.1, bf16[16,3584]{1,0:T(8,128)(2,1)} %refs_1_.1, bf16[16,64,512]{2,1,0:T(8,128)(2,1)} %refs_2_.1, bf16[16,4096]{1,0:T(8,128)(2,1)} %refs_3_.1, bf16[16,128,512]{2,1,0:T(8,128)(2,1)} %refs_4_.1, bf16[16,64,128]{2,1,0:T(8,128)(2,1)} %refs_5_.1, bf16[512,1024]{1,0:T(8,128)(2,1)} %refs_6_.1, ...), custom_call_target="tpu_custom_call" | custom-call | tf_op jit(solution)/shard_map/layer/pallas_call | solution.py:487
  71.5 1.6 %copy.15 = bf16[16,3584]{1,0:T(8,128)(2,1)} copy(bf16[16,3584]{1,0:T(8,128)(2,1)} %layer.1) | data formatting | bytes 229376

commit v4 on v3

--- a/solution.py
+++ b/solution.py
@@ -23,7 +23,7 @@
 DIMS = ((0, 1, 2), (1, 2, 0), (2, 0, 1))
 CHUNKS = ((0, 512, 2), (512, 512, 0), (1024, 512, 1), (1536, 384, 2), (1920, 384, 0), (2304, 384, 1), (2688, 256, 2), (2944, 384, 0), (3328, 256, 1))
 WIDTHS = tuple(n for _, n, _ in CHUNKS[:-1]) + (CHUNKS[-1][1] + 128,)
-BACK = ((0, 512, 2), (512, 512, 0), (1024, 512, 1), (1536, 384, 2), (1920, 384, 0), (2304, 384, 1), (2688, 256, 2), (2944, 384, 0), (3328, 256, 1))
+BACK = ((0, 256, 2), (256, 256, 0), (512, 256, 1), (768, 512, 2), (1280, 512, 0), (1792, 512, 1), (2304, 384, 2), (2688, 512, 0), (3200, 384, 1))
 STRIDE = (32, 1, 8)
 
 
@@ -486,12 +486,12 @@
     anyspace = pl.BlockSpec(memory_space=pl.ANY)
     return pl.pallas_call(
         layer_kernel,
-        out_shape=jax.ShapeDtypeStruct((TOK, D), BF16),
+        out_shape=pltpu.VMEM((TOK, D), BF16),
         in_specs=[pl.BlockSpec(memory_space=pltpu.SMEM)] + [anyspace] * 12,
         out_specs=pl.BlockSpec(memory_space=pltpu.VMEM),
         scratch_shapes=scratch,
         compiler_params=pltpu.CompilerParams(
-            collective_id=0, has_side_effects=True, vmem_limit_bytes=64 * 1024 * 1024 - 65536
+            collective_id=0, has_side_effects=True, vmem_limit_bytes=62 * 1024 * 1024
         ),
         name="layer",
     )(

time: 73.1 us -> 71.5 us (0.978)
  local copies, waits for them, and re-layouts: 1.55 us -> 0.65 us
  Pallas kernels: 71.5 us -> 70.7 us
    unnamed x1, local copies, waits for them, and re-layouts: 1.55 us -> 0.65 us
where the time goes in v4:
time: 71.5 us; the launch traced here: 71.4 us
  Pallas kernels  70.7 us (99%)
    pallas_call x1, Pallas kernels, per_device(): pl.pallas_call(layer_kernel, out_shape=pltpu.VMEM((TOK, D), BF16), in_spe...  70.7 us

profile of v4, /device:TPU:1, one launch (start us, length us, event | category | flops | bytes accessed | tf_op | source)
XLA Modules:
  0.0 71.4 jit_solution(17253569724915767538)
XLA Ops:
  0.0 70.7 %layer.1 = bf16[16,3584]{1,0:T(8,128)(2,1)S(1)} custom-call(s32[16]{0:T(128)} %refs_0_.1, bf16[16,3584]{1,0:T(8,128)(2,1)} %refs_1_.1, bf16[16,64,512]{2,1,0:T(8,128)(2,1)} %refs_2_.1, bf16[16,4096]{1,0:T(8,128)(2,1)} %refs_3_.1, bf16[16,128,512]{2,1,0:T(8,128)(2,1)} %refs_4_.1, bf16[16,64,128]{2,1,0:T(8,128)(2,1)} %refs_5_.1, bf16[512,1024]{1,0:T(8,128)(2,1)} %refs_6_.1, ...), custom_call_target="tpu_custom_call" | custom-call | tf_op jit(solution)/shard_map/layer/pallas_call | solution.py:487
  70.7 0.6 copy.15
